TPU v7x, 256 devices: a whole 4x4x8 slice. The times are simulated.
256 devices in a mesh: basin: 8 (over z), reach: 32 (over x, y, core).
Axes of the slice: x: 4, y: 4, z: 8, core: 2. Of those that a mesh axis runs over, the one named last changes fastest.
Arguments:
- sensitivity: float32 [16, 1024, 256], P(None, ('basin', 'reach')), may hold values from -6 to 6
- inverse: float32 [1024, 256, 256], P(('basin', 'reach')), may hold values from -0.375 to 0.375
- spread: float32 [1024, 256], P(('basin', 'reach')), may hold values from -3 to 3
- gather_weight: float32 [1024, 256], P(('basin', 'reach')), may hold values from -0.0234375 to 0.0234375
- retain: float32 [1024], P(('basin', 'reach')), may hold values from 0.9980469 to 1
- storage: float32 [1024, 256], P(('basin', 'reach')), may hold values from 0.2 to 0.6
- conf_source: int32 [256, 32, 64], P(('basin', 'reach')), may hold values from 0 to 1023
- conf_target: int32 [256, 32, 64], P(('basin', 'reach')), may hold values from 0 to 1023
- conf_weight: float32 [256, 32, 64], P(('basin', 'reach')), may hold values from 0.1 to 0.4
Outputs:
- adjoint: float32 [16, 1024, 256], P(None, ('basin', 'reach'))
All inputs are finite; a program needn't handle non-finite values.
Results may differ from a plain program's by a relative error of at most 0.00019.
Values sent between devices are 32-bit elements; how exact they have to be, the bound alone decides.
A program may use at most 64 MiB of HBM per device.

v0:
```python
import jax
import jax.numpy as jnp
from jax import lax
from jax.sharding import Mesh
from jax.sharding import PartitionSpec as P

REACH = ("reach_0", "reach_1", "reach_2")
BASIN_REACH = ("basin", "reach_0", "reach_1", "reach_2")


def copy_for_each(x, axis):
    copies = jnp.broadcast_to(x, (lax.axis_size(axis), *x.shape))
    return lax.all_to_all(copies, axis, split_axis=0, concat_axis=0, tiled=True)


def all_in_one(x, axis):
    leaves = jax.tree.leaves(x)
    order = sorted(range(len(leaves)), key=lambda k: -leaves[k].size)
    width = (1, *leaves[order[0]].shape)[-1]
    lines = [
        jnp.pad(leaves[k].reshape(-1), (0, -leaves[k].size % width)).reshape(-1, width)
        for k in order
    ]
    both, at, found = (copy_for_each(jnp.concatenate(lines), axis), 0, {})
    for k, line in zip(order, lines):
        section = both[:, at : at + len(line)].reshape(len(both), -1)
        found[k] = section[:, : leaves[k].size].reshape(-1, *leaves[k].shape)
        at += len(line)
    numbers = iter(range(len(leaves)))
    return jax.tree.map(lambda _: found[next(numbers)], x)


def folded_in_pairs(pieces, combine):
    while len(jax.tree.leaves(pieces)[0]) > 1:
        pieces = jax.vmap(combine)(
            *(jax.tree.map(lambda part: part[side::2], pieces) for side in (0, 1))
        )
    return jax.tree.map(lambda part: part[0], pieces)


def entering_2(x, axis, combine, identity):
    size, here = (lax.axis_size(axis), lax.axis_index(axis))
    passed = jnp.arange(size) > here

    def kept(part, zero, own):
        part = jnp.where(
            passed.reshape(-1, *(1 for _ in own.shape)), part, jnp.asarray(zero, own.dtype)
        )
        return part[::-1]

    pieces = all_in_one(x, axis)
    return folded_in_pairs(jax.tree.map(kept, pieces, identity, x), combine)


def from_root(x, axes, root):
    x = jnp.where(lax.axis_index(axes) == root, x, jnp.zeros_like(x))
    for axis in axes:
        x = lax.psum(x, axis)
    return x


def once_a_type(x, axis):
    leaves, found = (jax.tree.leaves(x), {})
    for leading, a in enumerate(leaves):
        if leading not in found:
            alike = [k for k, b in enumerate(leaves) if b.dtype == a.dtype]
            got = (
                all_in_one([leaves[k] for k in alike], axis)
                if len(alike) > 1
                else [copy_for_each(a, axis)]
            )
            for k, b in zip(alike, got):
                found[k] = b
    numbers = iter(range(len(leaves)))
    return jax.tree.map(lambda _: found[next(numbers)], x)


def entering_3(x, axis, combine, identity):
    size, here = (lax.axis_size(axis), lax.axis_index(axis))
    passed = jnp.arange(size) > here

    def kept(part, zero, own):
        part = jnp.where(
            passed.reshape(-1, *(1 for _ in own.shape)), part, jnp.asarray(zero, own.dtype)
        )
        return part[::-1]

    pieces = once_a_type(x, axis)
    return folded_in_pairs(jax.tree.map(kept, pieces, identity, x), combine)


def compose(earlier, later):
    return (later[0] * earlier[0], later[0] * earlier[1] + later[1])


def on_device(
    sensitivity,
    inverse,
    spread,
    gather_weight,
    retain,
    storage,
    conf_source,
    conf_target,
    conf_weight,
):
    blocks, reaches = spread.shape
    rows = blocks * reaches
    sources = conf_source[0]
    targets = conf_target[0].reshape(-1)
    weights = conf_weight[0]
    identity = (jnp.ones((), jnp.float32), jnp.zeros((), jnp.float32))
    asked = lax.all_to_all(sources, REACH, split_axis=0, concat_axis=0, tiled=True)

    def step(later, forcing_now):
        flat = later.reshape(rows)
        picked = flat[asked]
        values = lax.all_to_all(picked, REACH, split_axis=0, concat_axis=0, tiled=True)
        fan = jnp.zeros((rows,), jnp.float32).at[targets].add((values * weights).reshape(-1))
        forcing = forcing_now + storage * later + fan.reshape(blocks, reaches)
        local = jnp.einsum("bij,bi->bj", inverse, forcing, precision=lax.Precision.HIGHEST)
        feed = jnp.sum(gather_weight * local, axis=1)
        slope = jnp.ones((), jnp.float32)
        offset = jnp.zeros((), jnp.float32)
        for block in reversed(range(blocks)):
            offset = retain[block] * offset + feed[block]
            slope = retain[block] * slope
        within = entering_2((slope, offset), REACH, compose, identity)
        inclusive = jnp.stack(compose(within, (slope, offset)))
        total = from_root(inclusive, REACH, 0)
        outer = entering_3((total[0], total[1]), "basin", compose, identity)
        prior = compose(outer, within)
        stem = prior[1]
        entering = []
        for block in reversed(range(blocks)):
            entering.append(stem)
            stem = retain[block] * stem + feed[block]
        stem_next = jnp.stack(entering[::-1])
        adjoint = local + spread * stem_next[:, None]
        return (adjoint, adjoint)

    _, adjoint = lax.scan(
        step, jnp.zeros((blocks, reaches), jnp.float32), sensitivity, reverse=True
    )
    return adjoint


def solution(mesh):
    torus = Mesh(
        mesh.devices.reshape(mesh.shape["basin"], 4, 4, 2),
        ("basin", "reach_0", "reach_1", "reach_2"),
    )
    placed = (
        P(None, BASIN_REACH, None),
        P(BASIN_REACH, None, None),
        P(BASIN_REACH, None),
        P(BASIN_REACH, None),
        P(BASIN_REACH),
        P(BASIN_REACH, None),
        P(BASIN_REACH, None, None),
        P(BASIN_REACH, None, None),
        P(BASIN_REACH, None, None),
    )
    return jax.shard_map(
        on_device,
        mesh=torus,
        in_specs=placed,
        out_specs=P(None, BASIN_REACH, None),
        check_vma=False,
    )
```

profile of v0, /device:TPU:1, one launch (start us, length us, event | category | flops | bytes accessed | tf_op | source)
XLA Modules:
  0.0 1682.4 jit_solution(13125824094660153234)
XLA Ops:
  0.0 8.7 all-to-all-start.3
  16.3 1665.4 %while.18 = (s32[]{:T(128)}, f32[4,256]{1,0:T(4,128)S(1)}, f32[16,4,256]{2,1,0:T(4,128)S(1)}, f32[16,4,256]{2,1,0:T(4,128)}, f32[4,256]{1,0:T(4,128)S(1)}, /*ind...) while((s32[]{:T(128)}, f32[4,256]{1,0:T(4,128)S(1)}, ...), condition=%wide.wide.region_6.7_spmd.clone, body=%wide.wide.region_0.6_spmd.clone.sunk | while | flops 3173677 | bytes 5576806 | solution.py:142
  16.4 8.6 gather_fusion
  38.3 14.7 scatter_custom_fusion.8
  64.4 7.0 all-to-all-done.1
  85.0 6.9 psum.49
  101.2 8.2 all-to-all-start.2
  124.5 8.6 gather_fusion
  147.3 14.7 scatter_custom_fusion.8
  173.4 7.0 all-to-all-done.1
  194.0 6.9 psum.49
  228.6 8.6 gather_fusion
  251.1 14.7 scatter_custom_fusion.8
  277.2 7.0 all-to-all-done.1
  297.8 6.9 psum.49
  332.4 8.6 gather_fusion
  354.9 14.7 scatter_custom_fusion.8
  381.0 7.0 all-to-all-done.1
  401.7 6.9 psum.49
  436.2 8.6 gather_fusion
  458.7 14.7 scatter_custom_fusion.8
  484.8 7.0 all-to-all-done.1
  505.5 6.9 psum.49
  540.0 8.6 gather_fusion
  562.5 14.7 scatter_custom_fusion.8
  588.6 7.0 all-to-all-done.1
  609.3 6.9 psum.49
  643.8 8.6 gather_fusion
  666.3 14.7 scatter_custom_fusion.8
  692.4 7.0 all-to-all-done.1
  713.1 6.9 psum.49
  747.6 8.6 gather_fusion
  770.1 14.7 scatter_custom_fusion.8
  796.2 7.0 all-to-all-done.1
  816.9 6.9 psum.49
  851.4 8.6 gather_fusion
  874.0 14.7 scatter_custom_fusion.8
  900.1 7.0 all-to-all-done.1
  920.7 6.9 psum.49
  955.2 8.6 gather_fusion
  977.8 14.7 scatter_custom_fusion.8
  1003.9 7.0 all-to-all-done.1
  1024.5 6.9 psum.49
  1059.0 8.6 gather_fusion
  1081.6 14.7 scatter_custom_fusion.8
  1107.7 7.0 all-to-all-done.1
  1128.3 6.9 psum.49
  1162.8 8.6 gather_fusion
  1185.4 14.7 scatter_custom_fusion.8
  1211.5 7.0 all-to-all-done.1
  1232.1 6.9 psum.49
  1266.6 8.6 gather_fusion
  1289.2 14.7 scatter_custom_fusion.8
  1315.3 7.0 all-to-all-done.1
  1370.4 8.6 gather_fusion
  1393.0 14.7 scatter_custom_fusion.8
  1419.1 7.0 all-to-all-done.1
  1474.2 8.6 gather_fusion
  1496.8 14.7 scatter_custom_fusion.8
  1522.9 7.0 all-to-all-done.1
  1578.0 8.6 gather_fusion
  1600.6 14.7 scatter_custom_fusion.8
  1626.7 7.0 all-to-all-done.1
  1647.3 6.9 psum.49
  (1318 shorter events, 876.2 us)
Async XLA Ops:
  0.0 15.6 all-to-all-start.3
  25.7 11.3 all-to-all-start
  60.2 11.2 all-to-all-start.1
  101.2 14.7 all-to-all-start.2
  124.5 38.2 %copy-start = (f32[4,256,256]{2,1,0:T(8,128)S(1)}, f32[4,256,256]{2,1,0:T(8,128)}, u32[]{:S(2)}) copy-start(f32[4,256,256]{2,1,0:T(8,128)} %get-tuple-element.697) | copy-start | bytes 3145732 | tf_op jit(solution)/shard_map/while
  133.8 12.3 all-to-all-start
  169.3 11.2 all-to-all-start.1
  210.3 9.7 all-to-all-start.2
  228.6 37.9 %copy-start = (f32[4,256,256]{2,1,0:T(8,128)S(1)}, f32[4,256,256]{2,1,0:T(8,128)}, u32[]{:S(2)}) copy-start(f32[4,256,256]{2,1,0:T(8,128)} %get-tuple-element.697) | copy-start | bytes 3145732 | tf_op jit(solution)/shard_map/while
  237.8 12.0 all-to-all-start
  273.1 11.2 all-to-all-start.1
  314.1 9.7 all-to-all-start.2
  332.4 37.9 %copy-start = (f32[4,256,256]{2,1,0:T(8,128)S(1)}, f32[4,256,256]{2,1,0:T(8,128)}, u32[]{:S(2)}) copy-start(f32[4,256,256]{2,1,0:T(8,128)} %get-tuple-element.697) | copy-start | bytes 3145732 | tf_op jit(solution)/shard_map/while
  341.7 12.0 all-to-all-start
  376.9 11.2 all-to-all-start.1
  417.9 9.7 all-to-all-start.2
  436.2 37.9 %copy-start = (f32[4,256,256]{2,1,0:T(8,128)S(1)}, f32[4,256,256]{2,1,0:T(8,128)}, u32[]{:S(2)}) copy-start(f32[4,256,256]{2,1,0:T(8,128)} %get-tuple-element.697) | copy-start | bytes 3145732 | tf_op jit(solution)/shard_map/while
  445.5 12.0 all-to-all-start
  480.7 11.2 all-to-all-start.1
  521.7 9.7 all-to-all-start.2
  540.0 37.9 %copy-start = (f32[4,256,256]{2,1,0:T(8,128)S(1)}, f32[4,256,256]{2,1,0:T(8,128)}, u32[]{:S(2)}) copy-start(f32[4,256,256]{2,1,0:T(8,128)} %get-tuple-element.697) | copy-start | bytes 3145732 | tf_op jit(solution)/shard_map/while
  549.3 12.0 all-to-all-start
  584.5 11.2 all-to-all-start.1
  625.5 9.7 all-to-all-start.2
  643.8 37.9 %copy-start = (f32[4,256,256]{2,1,0:T(8,128)S(1)}, f32[4,256,256]{2,1,0:T(8,128)}, u32[]{:S(2)}) copy-start(f32[4,256,256]{2,1,0:T(8,128)} %get-tuple-element.697) | copy-start | bytes 3145732 | tf_op jit(solution)/shard_map/while
  653.1 12.0 all-to-all-start
  688.3 11.2 all-to-all-start.1
  729.3 9.7 all-to-all-start.2
  747.6 37.9 %copy-start = (f32[4,256,256]{2,1,0:T(8,128)S(1)}, f32[4,256,256]{2,1,0:T(8,128)}, u32[]{:S(2)}) copy-start(f32[4,256,256]{2,1,0:T(8,128)} %get-tuple-element.697) | copy-start | bytes 3145732 | tf_op jit(solution)/shard_map/while
  756.9 12.0 all-to-all-start
  792.1 11.2 all-to-all-start.1
  833.1 9.7 all-to-all-start.2
  851.4 37.9 %copy-start = (f32[4,256,256]{2,1,0:T(8,128)S(1)}, f32[4,256,256]{2,1,0:T(8,128)}, u32[]{:S(2)}) copy-start(f32[4,256,256]{2,1,0:T(8,128)} %get-tuple-element.697) | copy-start | bytes 3145732 | tf_op jit(solution)/shard_map/while
  860.7 12.0 all-to-all-start
  895.9 11.2 all-to-all-start.1
  936.9 9.7 all-to-all-start.2
  955.2 37.9 %copy-start = (f32[4,256,256]{2,1,0:T(8,128)S(1)}, f32[4,256,256]{2,1,0:T(8,128)}, u32[]{:S(2)}) copy-start(f32[4,256,256]{2,1,0:T(8,128)} %get-tuple-element.697) | copy-start | bytes 3145732 | tf_op jit(solution)/shard_map/while
  964.5 12.0 all-to-all-start
  999.7 11.2 all-to-all-start.1
  1040.7 9.7 all-to-all-start.2
  1059.0 37.9 %copy-start = (f32[4,256,256]{2,1,0:T(8,128)S(1)}, f32[4,256,256]{2,1,0:T(8,128)}, u32[]{:S(2)}) copy-start(f32[4,256,256]{2,1,0:T(8,128)} %get-tuple-element.697) | copy-start | bytes 3145732 | tf_op jit(solution)/shard_map/while
  1068.3 12.0 all-to-all-start
  1103.5 11.2 all-to-all-start.1
  1144.5 9.7 all-to-all-start.2
  1162.8 37.9 %copy-start = (f32[4,256,256]{2,1,0:T(8,128)S(1)}, f32[4,256,256]{2,1,0:T(8,128)}, u32[]{:S(2)}) copy-start(f32[4,256,256]{2,1,0:T(8,128)} %get-tuple-element.697) | copy-start | bytes 3145732 | tf_op jit(solution)/shard_map/while
  1172.1 12.0 all-to-all-start
  1207.3 11.2 all-to-all-start.1
  1248.3 9.7 all-to-all-start.2
  1266.6 37.9 %copy-start = (f32[4,256,256]{2,1,0:T(8,128)S(1)}, f32[4,256,256]{2,1,0:T(8,128)}, u32[]{:S(2)}) copy-start(f32[4,256,256]{2,1,0:T(8,128)} %get-tuple-element.697) | copy-start | bytes 3145732 | tf_op jit(solution)/shard_map/while
  1275.9 12.0 all-to-all-start
  1311.1 11.2 all-to-all-start.1
  1352.1 9.7 all-to-all-start.2
  1370.4 37.9 %copy-start = (f32[4,256,256]{2,1,0:T(8,128)S(1)}, f32[4,256,256]{2,1,0:T(8,128)}, u32[]{:S(2)}) copy-start(f32[4,256,256]{2,1,0:T(8,128)} %get-tuple-element.697) | copy-start | bytes 3145732 | tf_op jit(solution)/shard_map/while
  1379.7 12.0 all-to-all-start
  1414.9 11.2 all-to-all-start.1
  1455.9 9.7 all-to-all-start.2
  1474.2 37.9 %copy-start = (f32[4,256,256]{2,1,0:T(8,128)S(1)}, f32[4,256,256]{2,1,0:T(8,128)}, u32[]{:S(2)}) copy-start(f32[4,256,256]{2,1,0:T(8,128)} %get-tuple-element.697) | copy-start | bytes 3145732 | tf_op jit(solution)/shard_map/while
  1483.5 12.0 all-to-all-start
  1518.7 11.2 all-to-all-start.1
  1559.7 9.7 all-to-all-start.2
  1578.0 37.9 %copy-start = (f32[4,256,256]{2,1,0:T(8,128)S(1)}, f32[4,256,256]{2,1,0:T(8,128)}, u32[]{:S(2)}) copy-start(f32[4,256,256]{2,1,0:T(8,128)} %get-tuple-element.697) | copy-start | bytes 3145732 | tf_op jit(solution)/shard_map/while
  1587.3 12.0 all-to-all-start
  1622.5 11.2 all-to-all-start.1
  1663.5 9.7 all-to-all-start.2
  (8 other events, 61.8 us)
where the time goes:
time: 1690 us; the launch traced here: 1680 us
  blocking collectives  327 us (19%)
  waiting for transfers between devices  318 us (19%)
  local copies, waits for them, and re-layouts  312 us (18%)
  other arithmetic  287 us (17%)
  loops' own time  213 us (13%)
  starting transfers between devices  212 us (13%)
    psum x48, blocking collectives, from_root(): x = lax.psum(x, axis)  327 us
    scatter-add x16, other arithmetic, step(): jnp.zeros((rows,), jnp.float32).at[targets]  235 us
    all_to_all x32, waiting for transfers between devices, copy_for_each(): return lax.all_to_all(copies, axis, split_axis=0, concat_axis=0, tiled=True)  214 us
    another operation x1, loops' own time, on_device(): lax.scan(step, jnp.zeros((blocks, reaches), jnp.float32), sensitivity, re...  213 us
    gather x16, local copies, waits for them, and re-layouts, step(): picked = flat[asked]  137 us
    all_to_all x32, starting transfers between devices, copy_for_each(): return lax.all_to_all(copies, axis, split_axis=0, concat_axis=0, tiled=True)  124 us
    all_to_all x16, waiting for transfers between devices, step(): lax.all_to_all(picked, REACH, split_axis=0, concat_axis=0, tiled=True)  101 us
    slice x576, local copies, waits for them, and re-layouts, folded_in_pairs(): part[side::2]  88.1 us
  transfers between devices with their start and end apart: 49, of which 49 were waited for; matrix products, arithmetic and copies ran while one was open for 1% of the time, Pallas kernels for 0%

commit v1 on v0

v1 whole, which is shorter than its diff:
```python
import functools

import jax
import jax.numpy as jnp
from jax import lax
from jax.experimental import pallas as pl
from jax.experimental.pallas import tpu as pltpu
from jax.sharding import PartitionSpec as P

LANES = 128
MESH = pl.DeviceIdType.MESH


def lane_take(row, index):
    return jnp.take_along_axis(jnp.broadcast_to(row, index.shape), index, axis=1)


def split_halves(x):
    return jnp.concatenate([x[:, :LANES], x[:, LANES:]], axis=0)


def place(j):
    return ((j >> 7) & 1) * 4 + (j >> 8), j & 127


def kernel(
    basins, peers, steps,
    sens_ref, inv_ref, spread_ref, gather_ref, retain_ref, storage_ref,
    source_ref, target_ref, weight_ref,
    out_ref,
    send_buf, recv_buf, once_send, once_recv, z_send, z_recv,
    coef_ref, hot_ref, mask_ref,
    send_sem, recv_sem, once_send_sem, once_recv_sem, z_send_sem, z_recv_sem,
):
    g = lax.axis_index("basin")
    me = lax.axis_index("reach")
    half = peers // 2
    f32 = jnp.float32

    if peers == 32:
        x, y, c = me // 8, (me // 2) % 4, me % 2
        hop = (0, 1, 2, 1)
        order = sorted(
            ((dx, dy, dc) for dx in range(4) for dy in range(4) for dc in range(2)),
            key=lambda d: -(hop[d[0]] + hop[d[1]]) * 2 - d[2],
        )
        others = [
            (((x + dx) % 4) * 4 + (y + dy) % 4) * 2 + (c + dc) % 2
            for dx, dy, dc in order
            if (dx, dy, dc) != (0, 0, 0)
        ]
    else:
        others = [(me + d) % peers for d in range(1, peers)]

    barrier = pltpu.get_barrier_semaphore()
    for p in others:
        pl.semaphore_signal(barrier, inc=1, device_id={"reach": p}, device_id_type=MESH)

    @pl.when(g > 0)
    def _():
        pl.semaphore_signal(barrier, inc=1, device_id={"basin": g - 1}, device_id_type=MESH)

    @pl.when(g < basins - 1)
    def _():
        pl.semaphore_signal(barrier, inc=1, device_id={"basin": g + 1}, device_id_type=MESH)

    lane = lax.broadcasted_iota(jnp.int32, (peers, LANES), 1)
    row = lax.broadcasted_iota(jnp.int32, (peers, LANES), 0)
    low = lane < 64
    low_half = low[:half]
    lane8 = lax.broadcasted_iota(jnp.int32, (8, LANES), 1)
    row8 = lax.broadcasted_iota(jnp.int32, (8, LANES), 0)
    block8 = row8 % 4

    r0, r1, r2, r3 = (retain_ref[i] for i in range(4))
    slope_me = r0 * r1 * r2 * r3

    first = jnp.concatenate(
        [source_ref[0].astype(f32), jnp.full((peers, 64), slope_me, f32)], axis=1
    )
    once_send[0] = first.reshape(peers, 1, LANES)
    once_recv[0, pl.ds(me, 1)] = once_send[0, pl.ds(me, 1)]

    neighbours = (g > 0).astype(jnp.int32) + (g < basins - 1).astype(jnp.int32)
    pl.semaphore_wait(barrier, peers - 1 + neighbours)

    def to_all(src, dst, s_sem, r_sem):
        for p in others:
            pltpu.make_async_remote_copy(
                src_ref=src.at[pl.ds(p, 1)], dst_ref=dst.at[pl.ds(me, 1)],
                send_sem=s_sem, recv_sem=r_sem,
                device_id={"reach": p}, device_id_type=MESH,
            ).start()

    def all_done(buf, sem):
        part = buf.at[pl.ds(0, peers - 1)]
        pltpu.make_async_copy(part, part, sem).wait()

    to_all(once_send.at[0], once_recv.at[0], once_send_sem.at[0], once_recv_sem.at[0])

    @pl.when(g == basins - 1)
    def _():
        z_recv[...] = jnp.zeros_like(z_recv)

    spread = split_halves(spread_ref[...])
    storage = split_halves(storage_ref[...])
    keep = [
        jnp.where(block8 == 0, a, jnp.where(block8 == 1, b, jnp.where(block8 == 2, d, e)))
        for a, b, d, e in (
            (1.0, r0, r0 * r1, r0 * r1 * r2),
            (1.0, 1.0, 1.0, 0.0),
            (r1, r2, 0.0, 0.0),
            (r1 * r2, 0.0, 0.0, 0.0),
            (r1 * r2 * r3, r2 * r3, r3, 1.0),
        )
    ]
    spread_in = spread * keep[4]

    target = jnp.concatenate([target_ref[0, :half], target_ref[0, half:]], axis=1)
    weight = jnp.concatenate([weight_ref[0, :half], weight_ref[0, half:]], axis=1)
    t_row, t_lane = place(target)
    sub = lax.broadcasted_iota(jnp.int32, (LANES, LANES), 0)
    for q in range(half):
        mask_ref[q] = jnp.where(row8 == t_row[q : q + 1], weight[q : q + 1], 0.0)
        hot = jnp.where(sub == t_lane[q : q + 1], 1.0, 0.0)
        hot_ref[q * LANES : (q + 1) * LANES, :] = hot.T.astype(jnp.bfloat16)

    feed_row = split_halves(
        jnp.concatenate(
            [
                lax.dot_general(
                    gather_ref[b : b + 1], inv_ref[b], (((1,), (1,)), ((), ())),
                    precision=lax.Precision.HIGHEST, preferred_element_type=f32,
                )
                for b in range(4)
            ],
            axis=0,
        )
    )

    all_done(once_recv.at[0], once_recv_sem.at[0])
    got = once_recv[0].reshape(peers, LANES)
    asked_row, asked_lane = place(jnp.where(low, got, 0.0).astype(jnp.int32))
    slope = jnp.where(low, pltpu.roll(got, 64, 1), got)

    rest, d = slope, 1
    level = 0
    while d < peers:
        coef_ref[level] = jnp.where(row + d < peers, rest, 0.0)
        rest = rest * jnp.where(row + d < peers, pltpu.roll(rest, peers - d, 0), 1.0)
        d, level = 2 * d, level + 1
    levels = level
    past = jnp.where(row < peers - 1, pltpu.roll(rest, peers - 1, 0), 1.0)
    whole = rest[0:1]

    def picked(x):
        out = jnp.zeros((peers, LANES), f32)
        for r in range(8):
            out = jnp.where(asked_row == r, lane_take(x[r : r + 1], asked_lane), out)
        return out

    once_send[1] = picked(spread_in).reshape(peers, 1, LANES)
    once_recv[1, pl.ds(me, 1)] = once_send[1, pl.ds(me, 1)]

    column = lax.broadcasted_iota(jnp.int32, (LANES, LANES), 0)

    def advance(k, forcing):
        part = jnp.broadcast_to(
            jnp.sum(forcing * feed_row, axis=1, keepdims=True), (8, LANES)
        )
        feed = part + pltpu.roll(part, 4, 0)
        offset = jnp.sum(keep[0] * part, axis=0, keepdims=True)
        within = (
            keep[1] * pltpu.roll(feed, 7, 0)
            + keep[2] * pltpu.roll(feed, 6, 0)
            + keep[3] * pltpu.roll(feed, 5, 0)
        )
        sums = []
        for b in range(4):
            total = jnp.zeros((8, 2 * LANES), f32)
            for h in range(2):
                col = lane_take(forcing[h * 4 + b : h * 4 + b + 1], column)
                col = jnp.concatenate([col, col], axis=1)
                block = inv_ref[b, h * LANES : (h + 1) * LANES, :]
                total = total + jnp.sum((col * block).reshape(16, 8, 2 * LANES), axis=0)
            sums.append(jnp.sum(total, axis=0, keepdims=True))
        local = split_halves(jnp.concatenate(sums, axis=0))
        partial = local + spread * within
        message = jnp.where(low, picked(partial), jnp.broadcast_to(offset, (peers, LANES)))
        send_buf[k] = message.reshape(peers, 1, LANES)
        to_all(send_buf.at[k], recv_buf.at[k], send_sem.at[k], recv_sem.at[k])
        recv_buf[k, pl.ds(me, 1)] = send_buf[k, pl.ds(me, 1)]
        return partial

    def arrive(k, partial):
        all_done(recv_buf.at[k], recv_sem.at[k])
        rows = recv_buf[k].reshape(peers, LANES)
        turned = pltpu.roll(rows, 64, 1)
        stem = jnp.where(low, turned, rows)
        for level in range(levels):
            stem = stem + coef_ref[level] * pltpu.roll(stem, peers - 2**level, 0)

        @pl.when(g < basins - 1)
        def _():
            here = z_recv.at[k]
            pltpu.make_async_copy(here, here, z_recv_sem.at[k]).wait()

        outer = z_recv[k]

        @pl.when(g > 0)
        def _():
            z_send[k] = stem[0:1] + whole * outer
            pltpu.make_async_remote_copy(
                src_ref=z_send.at[k], dst_ref=z_recv.at[k],
                send_sem=z_send_sem.at[k], recv_sem=z_recv_sem.at[k],
                device_id={"basin": g - 1}, device_id_type=MESH,
            ).start()

        entering = jnp.where(row < peers - 1, pltpu.roll(stem, peers - 1, 0), 0.0)
        entering = entering + past * outer
        own = jnp.sum(jnp.where(row == me, entering, 0.0), axis=0, keepdims=True)
        adjoint = partial + spread_in * own
        t = steps - 1 - k
        out_ref[t, :, 0:LANES] = adjoint[0:4]
        out_ref[t, :, LANES : 2 * LANES] = adjoint[4:8]
        return rows, turned, entering, adjoint

    partial = advance(0, split_halves(sens_ref[steps - 1]))
    to_all(once_send.at[1], once_recv.at[1], once_send_sem.at[1], once_recv_sem.at[1])
    all_done(once_recv.at[1], once_recv_sem.at[1])
    got = once_recv[1].reshape(peers, LANES)
    spread_at = jnp.where(low_half, got[:half], pltpu.roll(got[half:], 64, 1))

    def body(k, partial):
        rows, turned, entering, adjoint = arrive(k - 1, partial)
        values = jnp.where(low_half, rows[:half], turned[half:])
        stems = jnp.where(low_half, entering[:half], entering[half:])
        values = values + spread_at * stems
        fan = jnp.zeros((16, LANES), f32)
        lines = []
        for q in range(half):
            line = values[q : q + 1] * mask_ref[q]
            coarse = line.astype(jnp.bfloat16).astype(f32)
            lines.append(jnp.concatenate([coarse, line - coarse], axis=0).astype(jnp.bfloat16))
        fan = jnp.dot(
            jnp.concatenate(lines, axis=1), hot_ref[...], preferred_element_type=f32
        )
        forcing = (
            split_halves(sens_ref[steps - 1 - k]) + storage * adjoint + (fan[0:8] + fan[8:16])
        )
        return advance(k, forcing)

    partial = lax.fori_loop(1, steps, body, partial)
    arrive(steps - 1, partial)

    for i in range(2):
        all_done(once_send.at[i], once_send_sem.at[i])

    def drain(k, carry):
        all_done(send_buf.at[k], send_sem.at[k])

        @pl.when(g > 0)
        def _():
            here = z_send.at[k]
            pltpu.make_async_copy(here, here, z_send_sem.at[k]).wait()

        return carry

    lax.fori_loop(0, steps, drain, 0)


def solution(mesh):
    basins, peers = mesh.shape["basin"], mesh.shape["reach"]
    both = ("basin", "reach")

    def on_device(*args):
        steps, blocks, reaches = args[0].shape
        vmem = pl.BlockSpec(memory_space=pltpu.VMEM)
        smem = pl.BlockSpec(memory_space=pltpu.SMEM)
        levels = max(1, (peers - 1).bit_length())
        dma = pltpu.SemaphoreType.DMA
        return pl.pallas_call(
            functools.partial(kernel, basins, peers, steps),
            out_shape=jax.ShapeDtypeStruct((steps, blocks, reaches), jnp.float32),
            in_specs=[vmem] * 4 + [smem] + [vmem] * 4,
            out_specs=vmem,
            scratch_shapes=[
                pltpu.VMEM((steps, peers, 1, LANES), jnp.float32),
                pltpu.VMEM((steps, peers, 1, LANES), jnp.float32),
                pltpu.VMEM((2, peers, 1, LANES), jnp.float32),
                pltpu.VMEM((2, peers, 1, LANES), jnp.float32),
                pltpu.VMEM((steps, 1, LANES), jnp.float32),
                pltpu.VMEM((steps, 1, LANES), jnp.float32),
                pltpu.VMEM((levels, peers, LANES), jnp.float32),
                pltpu.VMEM((peers // 2 * LANES, LANES), jnp.bfloat16),
                pltpu.VMEM((peers // 2, 8, LANES), jnp.float32),
                dma((steps,)), dma((steps,)), dma((2,)), dma((2,)),
                dma((steps,)), dma((steps,)),
            ],
            compiler_params=pltpu.CompilerParams(collective_id=0, has_side_effects=True),
        )(*args)

    two, three = P(both, None), P(both, None, None)
    return jax.shard_map(
        on_device,
        mesh=mesh,
        in_specs=(P(None, both, None), three, two, two, P(both), two, three, three, three),
        out_specs=P(None, both, None),
        check_vma=False,
    )
```

time: 1690 us -> 123 us (0.07)
  blocking collectives: 327 us -> 0 us
  waiting for transfers between devices: 318 us -> 0 us
  local copies, waits for them, and re-layouts: 312 us -> 1.47 us
  other arithmetic: 287 us -> 0 us
  loops' own time: 213 us -> 0 us
  starting transfers between devices: 212 us -> 0 us
  Pallas kernels: 0 us -> 121 us
    psum x48 -> x0, blocking collectives: 327 us -> none  [from_root(): x = lax.psum(x, axis)]
    all_to_all x49 -> x0, waiting for transfers between devices: 318 us -> none  [the longest x32 214 us: copy_for_each(): return lax.all_to_all(copies, axis, split_axis=0, concat_axis=0, tiled=True)]
    scatter-add x16 -> x0, other arithmetic: 235 us -> none  [step(): jnp.zeros((rows,), jnp.float32).at[targets]]
    another operation x1 -> x0, loops' own time: 213 us -> none  [on_device(): lax.scan(step, jnp.zeros((blocks, reaches), jnp.float32), sensitivity, re...]
    all_to_all x49 -> x0, starting transfers between devices: 212 us -> none  [the longest x32 124 us: copy_for_each(): return lax.all_to_all(copies, axis, split_axis=0, concat_axis=0, tiled=True)]
    gather x16 -> x0, local copies, waits for them, and re-layouts: 137 us -> none  [step(): picked = flat[asked]]
    slice x657 -> x0, local copies, waits for them, and re-layouts: 132 us -> none  [the longest x576 88.1 us: folded_in_pairs(): part[side::2]]
    pallas_call x0 -> x1, Pallas kernels: none -> 121 us  [on_device(): pl.pallas_call(functools.partial(kernel, basins, peers, steps), out_shape...]
  transfers between devices with their start and end apart: 49 -> 0, of which waited for: 49 -> 0; matrix products, arithmetic and copies ran while one was open for 1% -> 0% of each run, Pallas kernels for 0% -> 0%
where the time goes in v1:
time: 123 us; the launch traced here: 122 us
  Pallas kernels  121 us (98%)
  local copies, waits for them, and re-layouts  1.47 us (1%)
    pallas_call x1, Pallas kernels, on_device(): pl.pallas_call(functools.partial(kernel, basins, peers, steps), out_shape...  121 us

profile of v1, /device:TPU:1, one launch (start us, length us, event | category | flops | bytes accessed | tf_op | source)
XLA Modules:
  0.0 122.5 jit_solution(13089264104389936132)
XLA Ops:
  0.0 121.0 %shard_map.91 = f32[16,4,256]{2,1,0:T(4,128)} custom-call(f32[16,4,256]{2,1,0:T(4,128)} %sens_ref.1, f32[4,256,256]{2,1,0:T(8,128)} %inv_ref.1, f32[4,256]{1,0:T(4,128)} %spread_ref.1, f32[4,256]{1,0:T(4,128)} %gather_ref.1, f32[4]{0:T(128)} %retain_ref.1, f32[4,256]{1,0:T(4,128)} %storage_ref.1, s32[1,32,64]{2,1,0:T(8,128)} %source_ref.1, ...), custom_call_target="tpu_custom_call" | custom-call | tf_op jit(solution)/shard_map/pallas_call | solution.py:282
  121.0 1.5 %copy.11 = f32[16,4,256]{2,1,0:T(4,128)} copy(f32[16,4,256]{2,1,0:T(4,128)} %shard_map.91) | data formatting | bytes 131072
